TPU v7x, 32 devices: a whole 2x2x4 slice. The times are simulated.
32 devices in a mesh: ep: 16 (over z, y, x), opt: 2 (over core).
Axes of the slice: x: 2, y: 2, z: 4, core: 2. Of those that a mesh axis runs over, the one named last changes fastest.
Arguments:
- tokens: bfloat16 [2048, 2048], P('ep'), may hold values from -6 to 6
- out_grad: bfloat16 [2048, 2048], P('ep'), may hold values from -6 to 6
- expert_ids: int32 [2048, 2], P('ep'), may hold values from 0 to 15, all different within a row; in each aligned block of 128 rows (0 to 127, 128 to 255, ...) at most 32 rows name the same one
- route_gates: float32 [2048, 2], P('ep'), may hold values from 0.1 to 1
- gate_weight: bfloat16 [16, 2048, 512], P('ep', None, 'opt'), may hold values from -0.125 to 0.125
- up_weight: bfloat16 [16, 2048, 512], P('ep', None, 'opt'), may hold values from -0.125 to 0.125
- down_weight: bfloat16 [16, 512, 2048], P('ep', 'opt'), may hold values from -0.25 to 0.25
- momentum: float32 [16, 512, 2048], P('ep', 'opt'), may hold values from -80 to 80
Outputs:
- token_grad: bfloat16 [2048, 2048], P('ep', 'opt')
- new_momentum: float32 [16, 512, 2048], P('ep', 'opt')
- update: float32 [16, 512, 2048], P('ep', 'opt')
Inputs may be any that keep to these rules, and one draw needn't show every extreme that they name: `expert_ids`: within the rows of one index of ep, each expert is named at most 32 times, a bound that some block reaches; the 2 ids of a token differ.
All inputs are finite; a program needn't handle non-finite values.
Results may differ from a plain program's by a relative error of at most 0.011.
Values may be sent and summed in bfloat16 or wider, within the bound.
A program may use at most 64 MiB of HBM per device.

v0:
```python
import math

import jax
import jax.numpy as jnp
from jax import lax
from jax.sharding import PartitionSpec as P

NS_ITERS = 3


momentum_decay = 0.95
coeff_one = 3.4445
coeff_two = -4.775
coeff_three = 2.0315
epsilon = 1e-07


def slot_of_entries(flat_ids, experts_count, capacity):
    experts_all = jnp.arange(experts_count, dtype=jnp.int32)
    onehot = (flat_ids[:, None] == experts_all[None, :]).astype(jnp.int32)
    before = jnp.cumsum(onehot, axis=0) - onehot
    return flat_ids * capacity + jnp.sum(before * onehot, axis=1)


def combine_rows(returned, slots, token_count, topk_count):
    picked = returned[slots].astype(jnp.float32).reshape(token_count, topk_count, returned.shape[1])
    return jnp.sum(picked, axis=1).astype(jnp.bfloat16)


def gram_local(matrix):
    return lax.dot_general(
        matrix, matrix, (((1,), (1,)), ((), ())), preferred_element_type=jnp.float32
    )


def polynomial_step(gram_matrix, orthogonal):
    squared = jnp.dot(gram_matrix, gram_matrix, preferred_element_type=jnp.float32)
    polynomial = (coeff_two * gram_matrix.astype(jnp.float32) + coeff_three * squared).astype(
        jnp.bfloat16
    )
    product = jnp.dot(polynomial, orthogonal, preferred_element_type=jnp.float32)
    return (coeff_one * orthogonal.astype(jnp.float32) + product).astype(jnp.bfloat16)


def shards(
    tokens, out_grad, expert_ids, route_gates, gate_weight, up_weight, down_weight, momentum
):
    token_count = tokens.shape[0]
    topk_count = expert_ids.shape[1]
    model_width = tokens.shape[1]
    experts_count = lax.axis_size("ep")
    capacity = 2 * token_count * topk_count // experts_count
    flat_ids = expert_ids.reshape(-1)
    slots = slot_of_entries(flat_ids, experts_count, capacity)
    repeated = jnp.repeat(tokens, topk_count, axis=0)
    grad_rep = jnp.repeat(out_grad, topk_count, axis=0).astype(jnp.float32)
    scaled_rep = (route_gates.reshape(-1)[:, None] * grad_rep).astype(jnp.bfloat16)
    buffer_rows = experts_count * capacity
    part_width = model_width // lax.axis_size("opt")
    first_column = lax.axis_index("opt") * part_width
    part_inputs = lax.dynamic_slice_in_dim(repeated, first_column, part_width, 1)
    part_scaled = lax.dynamic_slice_in_dim(scaled_rep, first_column, part_width, 1)
    send_inputs = jnp.zeros((buffer_rows, part_width), jnp.bfloat16).at[slots].set(part_inputs)
    send_scaled = jnp.zeros((buffer_rows, part_width), jnp.bfloat16).at[slots].set(part_scaled)
    half_inputs, half_scaled = (
        lax.all_to_all(send_inputs, "ep", split_axis=0, concat_axis=0, tiled=True),
        lax.all_to_all(send_scaled, "ep", split_axis=0, concat_axis=0, tiled=True),
    )
    recv_inputs, recv_scaled = (
        lax.all_gather(half_inputs, "opt", axis=1, tiled=True),
        lax.all_gather(half_scaled, "opt", axis=1, tiled=True),
    )
    weight_gate = gate_weight[0]
    weight_up = up_weight[0]
    weight_down = down_weight[0]
    contract_last = (((1,), (1,)), ((), ()))
    pre_gate = jnp.dot(recv_inputs, weight_gate, preferred_element_type=jnp.float32)
    pre_up = jnp.dot(recv_inputs, weight_up, preferred_element_type=jnp.float32)
    sigmoid = jax.nn.sigmoid(pre_gate)
    activated = pre_gate * sigmoid
    hidden = (activated * pre_up).astype(jnp.bfloat16)
    hidden_grad = lax.dot_general(
        recv_scaled, weight_down, contract_last, preferred_element_type=jnp.float32
    )
    gate_grad = (hidden_grad * pre_up * sigmoid * (1.0 + pre_gate * (1.0 - sigmoid))).astype(
        jnp.bfloat16
    )
    up_grad = (hidden_grad * activated).astype(jnp.bfloat16)
    partial_grad = lax.dot_general(
        gate_grad, weight_gate, contract_last, preferred_element_type=jnp.float32
    ) + lax.dot_general(up_grad, weight_up, contract_last, preferred_element_type=jnp.float32)
    returned = lax.all_to_all(
        partial_grad.astype(jnp.bfloat16), "ep", split_axis=0, concat_axis=0, tiled=True
    ).astype(partial_grad.dtype)
    halves = lax.psum_scatter(returned.astype(jnp.bfloat16), "opt", scatter_dimension=1, tiled=True)
    token_grad = combine_rows(halves, slots, token_count, topk_count)
    down_grad = lax.dot_general(
        hidden, recv_scaled, (((0,), (0,)), ((), ())), preferred_element_type=jnp.float32
    )
    new_moment = momentum_decay * momentum[0] + down_grad
    squares = lax.psum(jnp.sum(new_moment * new_moment), "opt")
    initial = (new_moment / (jnp.sqrt(squares) + epsilon)).astype(jnp.bfloat16)
    row_count = initial.shape[0]
    orthogonal = lax.all_gather(initial, "opt", axis=0, tiled=True)
    for iteration in range(NS_ITERS):
        gram_matrix = gram_local(orthogonal).astype(jnp.bfloat16)
        orthogonal = polynomial_step(gram_matrix, orthogonal)
    own_rows = lax.dynamic_slice_in_dim(orthogonal, lax.axis_index("opt") * row_count, row_count, 0)
    update = math.sqrt(model_width) * own_rows.astype(jnp.float32)
    return (token_grad, new_moment[None], update[None])


def solution(mesh):
    in_specs = (
        P("ep", None),
        P("ep", None),
        P("ep", None),
        P("ep", None),
        P("ep", None, "opt"),
        P("ep", None, "opt"),
        P("ep", "opt", None),
        P("ep", "opt", None),
    )
    out_specs = (P("ep", "opt"), P("ep", "opt", None), P("ep", "opt", None))
    return jax.shard_map(shards, mesh=mesh, in_specs=in_specs, out_specs=out_specs, check_vma=False)
```

profile of v0, /device:TPU:14, one launch (start us, length us, event | category | flops | bytes accessed | tf_op | source)
XLA Modules:
  0.0 196.0 jit_solution(13682193524498902591)
XLA Ops:
  7.2 0.8 broadcast_multiply_fusion
  8.0 0.8 copy.12
  9.3 0.6 reduce-window.6
  10.1 1.7 broadcast_in_dim.17
  11.8 0.4 reshape.69
  12.4 1.9 scatter_custom_fusion.1
  14.3 31.3 %all_to_all.36 = bf16[16,32,1024]{2,1,0:T(8,128)(2,1)} all-to-all(bf16[16,32,1024]{2,1,0:T(8,128)(2,1)S(1)} %bitcast.70), channel_id=1, replica_groups=mesh['ep'=16,'opt'=2] {'ep'}, dimensions={0} | all-to-all | bytes 2097152 | tf_op jit(solution)/shard_map/all_to_all | solution.py:66
  45.7 2.1 %broadcast_in_dim.16 = f32[128,2,2048]{2,1,0:T(2,128)S(1)} broadcast(bf16[128,2048]{1,0:T(8,128)(2,1)} %param.9), dimensions={0,2} | broadcast | bytes 2621440 | tf_op jit(solution)/shard_map/broadcast_in_dim | solution.py:56
  47.8 2.4 %convert_element_type.88 = f32[256,2048]{1,0:T(8,128)} reshape(f32[128,2,2048]{2,1,0:T(2,128)S(1)} %broadcast_in_dim.16) | data formatting | bytes 4194304 | tf_op jit(solution)/shard_map/convert_element_type | solution.py:56
  50.5 2.7 %scatter_custom_fusion = bf16[512,1024]{1,0:T(8,128)(2,1)S(1)} fusion(s32[256]{0:T(256)S(1)} %bitcast.72, f32[256,2048]{1,0:T(8,128)} %convert_element_type.88, s32[]{:T(128)} %constant.18.clone.1, s32[]{:T(128)S(6)} %select_n.20, f32[256]{0:T(256)S(1)} %mul.105, bf16[]{:T(256)} %constant.16.clone.1), kind=kCustom, calls=%fused_computation.38 | custom fusion | flops 524288 | bytes 2099204 | tf_op jit(solution)/shard_map/scatter | solution.py:64
  53.2 29.4 %all_to_all.37 = bf16[16,32,1024]{2,1,0:T(8,128)(2,1)} all-to-all(bf16[16,32,1024]{2,1,0:T(8,128)(2,1)S(1)} %bitcast.69), channel_id=1, replica_groups=mesh['ep'=16,'opt'=2] {'ep'}, dimensions={0} | all-to-all | bytes 2097152 | tf_op jit(solution)/shard_map/all_to_all | solution.py:67
  82.7 2.5 %fusion.11 = f32[512,256]{1,0:T(8,128)S(1)} fusion(bf16[512,2048]{1,0:T(8,128)(2,1)} %all-gather.6.cloned.1.call-done, bf16[1,2048,256]{2,1,0:T(8,128)(2,1)S(1)} %copy-done), kind=kOutput, calls=%fused_computation.29 | convolution fusion | flops 536870912 | bytes 3670016 | tf_op jit(solution)/shard_map/dot_general | solution.py:77
  85.2 0.7 fusion.14
  85.9 7.7 %all-gather.4.cloned.1.call-done = bf16[512,2048]{1,0:T(8,128)(2,1)} async-done(((bf16[512,1024]{1,0:T(8,128)(2,1)}), bf16[512,2048]{1,0:T(8,128)(2,1)}) %all-gather.4.cloned.1.call-update) | async-done | bytes 2097168 | tf_op jit(solution)/shard_map/all_gather | solution.py:71
  93.6 2.6 %fusion.16 = f32[512,256]{1,0:T(8,128)S(1)} fusion(bf16[512,2048]{1,0:T(8,128)(2,1)} %all-gather.4.cloned.1.call-done, bf16[1,256,2048]{2,1,0:T(8,128)(2,1)} %param.14), kind=kOutput, calls=%fused_computation.34 | convolution fusion | flops 536870912 | bytes 3670016 | tf_op jit(solution)/shard_map/dot_general | solution.py:82
  96.2 0.9 fusion.9
  97.1 2.1 %add_convert_fusion.2 = bf16[512,2048]{1,0:T(8,128)(2,1)} fusion(f32[512,2048]{1,0:T(8,128)S(1)} %fusion.9, bf16[1,2048,256]{2,1,0:T(8,128)(2,1)S(1)} %copy-done.4, f32[512,256]{1,0:T(8,128)S(1)} %fusion.16, f32[512,256]{1,0:T(8,128)S(1)} %fusion.11), kind=kOutput, calls=%fused_computation.5 | convolution fusion | flops 539754496 | bytes 8388608 | tf_op jit(solution)/shard_map/dot_general | solution.py:91
  99.2 7.0 %all-to-all-start.2 = ((bf16[16,32,2048]{2,1,0:T(8,128)(2,1)}), bf16[16,32,2048]{2,1,0:T(8,128)(2,1)S(1)}, u32[]{:S(2)}, u32[]{:S(2)}) async-start(bf16[16,32,2048]{2,1,0:T(8,128)(2,1)} %bitcast.66), calls=%async_computation.2 | async-start | bytes 4194304 | tf_op jit(solution)/shard_map/all_to_all | solution.py:92
  106.2 5.3 %multiply_reduce_fusion = (f32[]{:T(128)}, f32[256,2048]{1,0:T(8,128)}) fusion(bf16[512,2048]{1,0:T(8,128)(2,1)} %all-gather.4.cloned.1.call-done, f32[512,256]{1,0:T(8,128)} %copy-done.3, f32[512,256]{1,0:T(8,128)} %copy-done.2, f32[1,256,2048]{2,1,0:T(8,128)} %param.15), kind=kOutput, calls=%fused_computation.11 | convolution fusion | flops 539754496 | bytes 7340036 | tf_op jit(solution)/shard_map/dot_general | solution.py:97
  111.5 3.1 %psum.7 = f32[]{:T(128)} all-reduce(f32[]{:T(128)} %get-tuple-element.3), channel_id=1, replica_groups=mesh['ep'=16,'opt'=2] {'opt'}, use_global_device_ids=true, to_apply=%region_8.9 | all-reduce | flops 1 | bytes 8 | tf_op jit(solution)/shard_map/psum | solution.py:101
  115.3 2.7 %divide_convert_fusion = bf16[256,2048]{1,0:T(8,128)(2,1)} fusion(f32[256,2048]{1,0:T(8,128)} %get-tuple-element.4, f32[]{:T(128)S(6)} %add.73), kind=kLoop, calls=%fused_computation.10 | loop fusion | flops 1048576 | bytes 3145732 | tf_op jit(solution)/shard_map/convert_element_type | solution.py:102
  118.3 36.4 %all-to-all-done.2 = bf16[16,32,2048]{2,1,0:T(8,128)(2,1)S(1)} async-done(((bf16[16,32,2048]{2,1,0:T(8,128)(2,1)}), bf16[16,32,2048]{2,1,0:T(8,128)(2,1)S(1)}, u32[]{:S(2)}, u32[]{:S(2)}) %all-to-all-start.2) | async-done | bytes 2097184 | tf_op jit(solution)/shard_map/all_to_all | solution.py:92
  154.6 1.3 copy-done.1
  156.0 4.5 %convolution_convert_fusion.2 = bf16[512,512]{1,0:T(8,128)(2,1)} fusion(bf16[512,2048]{1,0:T(8,128)(2,1)} %all-gather.8.cloned.1.call-done), kind=kOutput, calls=%fused_computation.23 | convolution fusion | flops 1074003968 | bytes 2621440 | tf_op jit(solution)/shard_map/dot_general | solution.py:31
  160.5 4.6 %add_convert_fusion.1 = bf16[512,2048]{1,0:T(8,128)(2,1)} fusion(bf16[512,2048]{1,0:T(8,128)(2,1)S(1)} %copy-done.6, bf16[512,512]{1,0:T(8,128)(2,1)} %convolution_convert_fusion.2), kind=kOutput, calls=%fused_computation.4 | convolution fusion | flops 1347682304 | bytes 4718592 | tf_op jit(solution)/shard_map/dot_general | solution.py:41
  165.1 4.3 %convolution_convert_fusion.1 = bf16[512,512]{1,0:T(8,128)(2,1)} fusion(bf16[512,2048]{1,0:T(8,128)(2,1)} %add_convert_fusion.1), kind=kOutput, calls=%fused_computation.22 | convolution fusion | flops 1074003968 | bytes 2621440 | tf_op jit(solution)/shard_map/dot_general | solution.py:31
  169.4 4.3 %add_convert_fusion = bf16[512,2048]{1,0:T(8,128)(2,1)S(1)} fusion(bf16[512,2048]{1,0:T(8,128)(2,1)} %add_convert_fusion.1, bf16[512,512]{1,0:T(8,128)(2,1)} %convolution_convert_fusion.1), kind=kOutput, calls=%fused_computation.3 | convolution fusion | flops 1347682304 | bytes 4718592 | tf_op jit(solution)/shard_map/dot_general | solution.py:41
  173.7 2.1 %convolution_convert_fusion = bf16[512,512]{1,0:T(8,128)(2,1)} fusion(bf16[512,2048]{1,0:T(8,128)(2,1)S(1)} %add_convert_fusion), kind=kOutput, calls=%fused_computation.21 | convolution fusion | flops 1074003968 | bytes 2621440 | tf_op jit(solution)/shard_map/dot_general | solution.py:31
  175.8 5.2 %fusion.7 = f32[512,2048]{1,0:T(8,128)} fusion(bf16[512,2048]{1,0:T(8,128)(2,1)S(1)} %add_convert_fusion, bf16[512,512]{1,0:T(8,128)(2,1)} %convolution_convert_fusion), kind=kOutput, calls=%fused_computation.24 | convolution fusion | flops 1343488000 | bytes 6815744 | tf_op jit(solution)/shard_map/dot_general | solution.py:41
  180.9 3.4 %multiply_bitcast_fusion = f32[1,256,2048]{2,1,0:T(8,128)} fusion(f32[512,2048]{1,0:T(8,128)} %fusion.7, s32[]{:T(128)S(6)} %select_n.21, bf16[512,2048]{1,0:T(8,128)(2,1)S(1)} %add_convert_fusion), kind=kLoop, calls=%fused_computation.9 | loop fusion | flops 3145728 | bytes 5242884 | tf_op jit(solution)/shard_map/broadcast_in_dim | solution.py:110
  184.3 2.9 %gather_fusion = bf16[256,1024]{1,0:T(8,128)(2,1)S(1)} fusion(bf16[512,1024]{1,0:T(8,128)(2,1)} %reduce-scatter.2.cloned.1.call-done, s32[1024]{0:T(1024)S(1)} %pad_clamp_fusion), kind=kCustom, calls=%fused_computation | custom fusion | bytes 1049600 | tf_op jit(solution)/shard_map/gather | solution.py:26
  187.4 2.1 %reduce_sum.34 = bf16[128,1024]{1,0:T(8,128)(2,1)} reduce(bf16[128,2,1024]{2,1,0:T(2,128)(2,1)S(1)} %gather.6, bf16[]{:T(256)} %constant.16.clone.1), dimensions={1}, to_apply=%region_6.7 | reduce | flops 131072 | bytes 786434 | tf_op jit(solution)/shard_map/reduce_sum | solution.py:27
  (40 shorter events, 1.8 us)
Async XLA Ops:
  7.2 75.5 %copy-start = (bf16[1,2048,256]{2,1,0:T(8,128)(2,1)S(1)}, bf16[1,2048,256]{2,1,0:T(8,128)(2,1)}, u32[]{:S(2)}) copy-start(bf16[1,2048,256]{2,1,0:T(8,128)(2,1)} %param.12) | copy-start | bytes 3145732
  7.2 75.5 %all-gather.6.cloned.1.call-start = ((), (), s32[]{:S(2)}) async-start(), calls=%async_computation.5 | async-start | bytes 3145728 | tf_op jit(solution)/shard_map/all_gather | solution.py:70
  45.6 48.0 %all-gather.4.cloned.1.call-start = ((), (), s32[]{:S(2)}) async-start(), calls=%async_computation.4 | async-start | bytes 3145728 | tf_op jit(solution)/shard_map/all_gather | solution.py:71
  47.8 2.5 %copy-start.5 = (f32[128,2]{0,1:T(2,128)S(1)}, f32[128,2]{0,1:T(2,128)}, u32[]{:S(2)}) copy-start(f32[128,2]{0,1:T(2,128)} %param.11) | copy-start | bytes 3076
  82.6 2.5 %copy-start.4 = (bf16[1,2048,256]{2,1,0:T(8,128)(2,1)S(1)}, bf16[1,2048,256]{2,1,0:T(8,128)(2,1)}, u32[]{:S(2)}) copy-start(bf16[1,2048,256]{2,1,0:T(8,128)(2,1)} %param.13) | copy-start | bytes 3145732
  82.7 2.5 %copy-start.7 = (bf16[512,2048]{1,0:T(8,128)(2,1)S(1)}, bf16[512,2048]{1,0:T(8,128)(2,1)}, u32[]{:S(2)}) copy-start(bf16[512,2048]{1,0:T(8,128)(2,1)} %all-gather.6.cloned.1.call-done) | copy-start | bytes 6291460
  85.2 11.9 %copy-start.2 = (f32[512,256]{1,0:T(8,128)}, f32[512,256]{1,0:T(8,128)S(1)}, u32[]{:S(2)}) copy-start(f32[512,256]{1,0:T(8,128)S(1)} %fusion.11) | copy-start | bytes 1572868
  85.9 10.3 %copy-start.3 = (f32[512,256]{1,0:T(8,128)}, f32[512,256]{1,0:T(8,128)S(1)}, u32[]{:S(2)}) copy-start(f32[512,256]{1,0:T(8,128)S(1)} %fusion.14) | copy-start | bytes 1572868
  99.2 55.4 %all-to-all-start.2 = ((bf16[16,32,2048]{2,1,0:T(8,128)(2,1)}), bf16[16,32,2048]{2,1,0:T(8,128)(2,1)S(1)}, u32[]{:S(2)}, u32[]{:S(2)}) async-start(bf16[16,32,2048]{2,1,0:T(8,128)(2,1)} %bitcast.66), calls=%async_computation.2 | async-start | bytes 4194304 | tf_op jit(solution)/shard_map/all_to_all | solution.py:92
  106.2 49.9 %all-gather.8.cloned.1.call-start = ((), (), s32[]{:S(2)}) async-start(), calls=%async_computation.7 | async-start | bytes 3145728 | tf_op jit(solution)/shard_map/all_gather | solution.py:104
  118.0 66.2 %reduce-scatter.2.cloned.1.call-start = ((), (), s32[]{:S(2)}) async-start(), calls=%async_computation.6 | async-start | bytes 3145728 | tf_op jit(solution)/shard_map/reduce_scatter | solution.py:95
  154.6 1.3 copy-start.1
  156.0 4.5 %copy-start.6 = (bf16[512,2048]{1,0:T(8,128)(2,1)S(1)}, bf16[512,2048]{1,0:T(8,128)(2,1)}, u32[]{:S(2)}) copy-start(bf16[512,2048]{1,0:T(8,128)(2,1)} %all-gather.8.cloned.1.call-done) | copy-start | bytes 6291460
Sparse Core Ops, SparseCore 0:
  45.7 10.7 all-gather.5
  82.7 10.8 all-gather.3
  118.1 11.6 all-gather.7
  156.1 9.1 reduce-scatter.1
where the time goes:
time: 197 us; the launch traced here: 196 us
  blocking collectives  63.8 us (32%)
  waiting for transfers between devices  44.2 us (22%)
  matrix products  38.9 us (20%)
  local copies, waits for them, and re-layouts  14.8 us (8%)
  between operations  14.7 us (7%)
  other arithmetic  12.4 us (6%)
  starting transfers between devices  7.29 us (4%)
    all_to_all x1, waiting for transfers between devices, shards(): lax.all_to_all(partial_grad.astype(jnp.bfloat16), 'ep', split_axis=0, con...  36.4 us
    all_to_all x1, blocking collectives, shards(): lax.all_to_all(send_inputs, 'ep', split_axis=0, concat_axis=0, tiled=True)  31.3 us
    all_to_all x1, blocking collectives, shards(): lax.all_to_all(send_scaled, 'ep', split_axis=0, concat_axis=0, tiled=True)  29.4 us
    dot_general x3, matrix products, polynomial_step(): jnp.dot(polynomial, orthogonal, preferred_element_type=jnp.float32)  14 us
    dot_general x3, matrix products, gram_local(): lax.dot_general(matrix, matrix, (((1,), (1,)), ((), ())), preferred_eleme...  10.8 us
    all_gather x1, waiting for transfers between devices, shards(): lax.all_gather(half_scaled, 'opt', axis=1, tiled=True)  7.7 us
    all_to_all x1, starting transfers between devices, shards(): lax.all_to_all(partial_grad.astype(jnp.bfloat16), 'ep', split_axis=0, con...  6.95 us
    dot_general x1, matrix products, shards(): lax.dot_general(hidden, recv_scaled, (((0,), (0,)), ((), ())), preferred_...  5.26 us
  transfers between devices with their start and end apart: 5, of which 2 were waited for; matrix products, arithmetic and copies ran while one was open for 24% of the time, Pallas kernels for 0%

commit v1 on v0

v1 whole, which is shorter than its diff:
```python
import functools
import math

import jax
import jax.numpy as jnp
from jax import lax
from jax.experimental import pallas as pl
from jax.experimental.pallas import tpu as pltpu
from jax.sharding import PartitionSpec as P

NS_ITERS = 3
MESH = pl.DeviceIdType.MESH

momentum_decay = 0.95
coeff_one = 3.4445
coeff_two = -4.775
coeff_three = 2.0315
epsilon = 1e-07

CONTRACT_LAST = (((1,), (1,)), ((), ()))
CONTRACT_FIRST = (((0,), (0,)), ((), ()))


def loop(count, body, start=0):
    def step(index, carry):
        body(index)
        return carry

    lax.fori_loop(start, count, step, 0)


def greet_all(peers, me, core):
    barrier = pltpu.get_barrier_semaphore()

    def greet(step):
        other = lax.rem(me + step, peers)
        pl.semaphore_signal(barrier, inc=1, device_id=(other, core), device_id_type=MESH)

    loop(peers, greet, 1)
    pl.semaphore_signal(barrier, inc=1, device_id=(me, 1 - core), device_id_type=MESH)
    pl.semaphore_wait(barrier, peers)


def dispatch_kernel(
    peers, send_first, send_second, out_first, out_second,
    local_sems, send_sems, recv_sems, push_sems, pull_sems,
):
    me, core = lax.axis_index("ep"), lax.axis_index("opt")
    part = send_first.shape[2]
    columns = pl.ds(pl.multiple_of(core * part, part), part)
    greet_all(peers, me, core)
    pairs = ((send_first, out_first), (send_second, out_second))

    def remote(which, other, source):
        send_ref, out_ref = pairs[which]
        return pltpu.make_async_remote_copy(
            src_ref=send_ref.at[other],
            dst_ref=out_ref.at[source, :, columns],
            send_sem=send_sems.at[which, other],
            recv_sem=recv_sems.at[which, source],
            device_id=(other, core),
            device_id_type=MESH,
        )

    def push(which, source, own):
        send_ref, out_ref = pairs[which]
        return pltpu.make_async_remote_copy(
            src_ref=send_ref.at[source] if own else out_ref.at[source, :, columns],
            dst_ref=out_ref.at[source, :, columns],
            send_sem=push_sems.at[which, source],
            recv_sem=pull_sems.at[which, source],
            device_id=(me, 1 - core),
            device_id_type=MESH,
        )

    other_columns = pl.ds(pl.multiple_of((1 - core) * part, part), part)

    def pull(which, source):
        out_ref = pairs[which][1]
        return pltpu.make_async_remote_copy(
            src_ref=out_ref.at[source, :, other_columns],
            dst_ref=out_ref.at[source, :, other_columns],
            send_sem=push_sems.at[which, source],
            recv_sem=pull_sems.at[which, source],
            device_id=(me, 1 - core),
            device_id_type=MESH,
        )

    for which in range(2):
        loop(peers, lambda step: remote(which, lax.rem(me + step, peers), me).start(), 1)
    for which in range(2):
        push(which, me, True).start()
        send_ref, out_ref = pairs[which]
        pltpu.make_async_copy(
            send_ref.at[me], out_ref.at[me, :, columns], local_sems.at[which]
        ).start()
    for which in range(2):

        def arrive(step):
            source = lax.rem(me + peers - step, peers)
            remote(which, source, source).wait_recv()
            push(which, source, False).start()

        loop(peers, arrive, 1)
    for which in range(2):
        send_ref, out_ref = pairs[which]
        pltpu.make_async_copy(
            send_ref.at[me], out_ref.at[me, :, columns], local_sems.at[which]
        ).wait()
        push(which, me, True).wait_send()

        def finish(step):
            source = lax.rem(me + peers - step, peers)
            remote(which, source, me).wait_send()
            push(which, source, False).wait_send()

        loop(peers, finish, 1)
        loop(peers, lambda source: pull(which, source).wait_recv())


def dispatch(send_first, send_second, peers, cores):
    _, rows, part = send_first.shape
    out = jax.ShapeDtypeStruct((peers, rows, part * cores), send_first.dtype)
    vmem = pl.BlockSpec(memory_space=pltpu.VMEM)
    sems = pltpu.SemaphoreType.DMA((2, peers))
    return pl.pallas_call(
        functools.partial(dispatch_kernel, peers),
        out_shape=(out, out),
        in_specs=[vmem] * 2,
        out_specs=(vmem, vmem),
        scratch_shapes=[pltpu.SemaphoreType.DMA((2,)), sems, sems, sems, sems],
        compiler_params=pltpu.CompilerParams(collective_id=0, has_side_effects=True),
        name="dispatch",
    )(send_first, send_second)


def return_kernel(
    peers, groups, partial, moment, squares, returned, ortho_out,
    extra, summed, other_squares, ortho, gram, gram_low, poly,
    send_sems, recv_sems, swap_send, swap_recv, misc_sems,
):
    me, core = lax.axis_index("ep"), lax.axis_index("opt")
    part = summed.shape[2]
    size = peers // groups
    own_rows, width = moment.shape
    all_rows = ortho.shape[0]
    own = pl.ds(pl.multiple_of(core * part, part), part)
    others = pl.ds(pl.multiple_of((1 - core) * part, part), part)
    greet_all(peers, me, core)
    mine = lax.div(me, size)

    def swap(step):
        first = lax.rem(mine + step, groups) * size
        return pltpu.make_async_remote_copy(
            src_ref=partial.at[pl.ds(first, size), :, others],
            dst_ref=extra.at[pl.ds(first, size)],
            send_sem=swap_send.at[step],
            recv_sem=swap_recv.at[step],
            device_id=(me, 1 - core),
            device_id_type=MESH,
        )

    def remote(other, source):
        return pltpu.make_async_remote_copy(
            src_ref=summed.at[other],
            dst_ref=returned.at[source],
            send_sem=send_sems.at[other],
            recv_sem=recv_sems.at[source],
            device_id=(other, core),
            device_id_type=MESH,
        )

    sums = pltpu.make_async_remote_copy(
        src_ref=squares,
        dst_ref=other_squares,
        send_sem=misc_sems.at[0],
        recv_sem=misc_sems.at[1],
        device_id=(me, 1 - core),
        device_id_type=MESH,
    )
    sums.start()
    loop(groups, lambda step: swap(step).start())
    sums.wait()
    frob = jnp.sqrt(squares[...] + other_squares[...])
    scale = (1.0 / (frob + epsilon))[0:1, 0:1]
    row_start = pl.multiple_of(core * own_rows, own_rows)
    row_tile = own_rows // 4

    def normalize(index):
        rows = pl.ds(pl.multiple_of(index * row_tile, row_tile), row_tile)
        target = pl.ds(pl.multiple_of(row_start + index * row_tile, row_tile), row_tile)
        ortho[target, :] = (moment[rows, :] * scale).astype(jnp.bfloat16)

    loop(4, normalize)

    def rows_copy(start):
        rows = pl.ds(pl.multiple_of(start, own_rows), own_rows)
        return pltpu.make_async_remote_copy(
            src_ref=ortho.at[rows],
            dst_ref=ortho.at[rows],
            send_sem=misc_sems.at[2],
            recv_sem=misc_sems.at[3],
            device_id=(me, 1 - core),
            device_id_type=MESH,
        )

    def leave(step):
        swap(step).wait_recv()
        first = lax.rem(mine + step, groups) * size

        def add(offset):
            other = first + offset
            total = partial[other, :, own].astype(jnp.float32) + extra[other].astype(jnp.float32)
            summed[other] = total.astype(jnp.bfloat16)

        def send(offset):
            other = first + offset

            @pl.when(other != me)
            def _():
                remote(other, me).start()

            @pl.when(other == me)
            def _():
                pltpu.make_async_copy(summed.at[me], returned.at[me], misc_sems.at[4]).start()

        loop(size, add)
        loop(size, send)

    loop(groups, leave)
    rows_copy(row_start).start()
    rows_copy((1 - core) * own_rows).wait_recv()
    rows_copy(row_start).wait_send()

    tile = min(512, width)
    tiles = width // tile

    def columns_of(index):
        return pl.ds(pl.multiple_of(index * tile, tile), tile)

    for iteration in range(NS_ITERS):
        gram[...] = jnp.zeros_like(gram)

        def grow(index):
            block = ortho[:, columns_of(index)]
            gram[...] += lax.dot_general(
                block, block, CONTRACT_LAST, preferred_element_type=jnp.float32
            )

        loop(tiles, grow)
        gram_low[...] = gram[...].astype(jnp.bfloat16)
        low = gram_low[...]
        squared = jnp.dot(low, low, preferred_element_type=jnp.float32)
        poly[...] = (coeff_two * low.astype(jnp.float32) + coeff_three * squared).astype(
            jnp.bfloat16
        )
        last = iteration == NS_ITERS - 1

        def apply(index):
            columns = columns_of(index)
            block = ortho[:, columns]
            if last:
                rows = pl.ds(row_start, own_rows)
                product = jnp.dot(poly[rows, :], block, preferred_element_type=jnp.float32)
                before = ortho[rows, columns].astype(jnp.float32)
                ortho_out[:, columns] = (coeff_one * before + product).astype(jnp.bfloat16)
            else:
                product = jnp.dot(poly[...], block, preferred_element_type=jnp.float32)
                ortho[:, columns] = (coeff_one * block.astype(jnp.float32) + product).astype(
                    jnp.bfloat16
                )

        loop(tiles, apply)

    pltpu.make_async_copy(summed.at[me], returned.at[me], misc_sems.at[4]).wait()

    def finish(step):
        other = lax.rem(me + step, peers)
        remote(other, me).wait_send()
        remote(other, other).wait_recv()

    loop(peers, finish, 1)
    loop(groups, lambda step: swap(step).wait_send())


def return_and_orthogonalize(partial, moment, squares, cores):
    peers, rows, width = partial.shape
    part = width // cores
    own_rows = moment.shape[0]
    all_rows = own_rows * cores
    groups = 4
    vmem = pl.BlockSpec(memory_space=pltpu.VMEM)
    dma = pltpu.SemaphoreType.DMA
    return pl.pallas_call(
        functools.partial(return_kernel, peers, groups),
        out_shape=(
            jax.ShapeDtypeStruct((peers, rows, part), jnp.bfloat16),
            jax.ShapeDtypeStruct((own_rows, width), jnp.bfloat16),
        ),
        in_specs=[vmem] * 3,
        out_specs=(vmem, vmem),
        scratch_shapes=[
            pltpu.VMEM((peers, rows, part), jnp.bfloat16),
            pltpu.VMEM((peers, rows, part), jnp.bfloat16),
            pltpu.VMEM(squares.shape, jnp.float32),
            pltpu.VMEM((all_rows, width), jnp.bfloat16),
            pltpu.VMEM((all_rows, all_rows), jnp.float32),
            pltpu.VMEM((all_rows, all_rows), jnp.bfloat16),
            pltpu.VMEM((all_rows, all_rows), jnp.bfloat16),
            dma((peers,)),
            dma((peers,)),
            dma((groups,)),
            dma((groups,)),
            dma((5,)),
        ],
        compiler_params=pltpu.CompilerParams(collective_id=1, has_side_effects=True),
        name="return_ortho",
    )(partial, moment, squares)


def placement(expert_ids, route_gates, slot_count, capacity):
    token_count, topk_count = expert_ids.shape
    earlier = (
        lax.broadcasted_iota(jnp.int32, (token_count, token_count), 0)
        < lax.broadcasted_iota(jnp.int32, (token_count, token_count), 1)
    )
    slot_iota = lax.broadcasted_iota(jnp.int32, (slot_count, token_count), 0)
    chosen = jnp.zeros((slot_count, token_count), jnp.bool_)
    gates = jnp.zeros((slot_count, token_count), jnp.float32)
    for k in range(topk_count):
        ids_row = expert_ids[:, k][None, :]
        same = jnp.zeros((token_count, token_count), jnp.bool_)
        for other in range(topk_count):
            same = same | (expert_ids[:, other][:, None] == ids_row)
        rank = jnp.sum((same & earlier).astype(jnp.int32), axis=0)
        hit = slot_iota == (expert_ids[:, k] * capacity + rank)[None, :]
        chosen = chosen | hit
        gates = gates + jnp.where(hit, route_gates[:, k][None, :], 0.0)
    return chosen.astype(jnp.bfloat16), jnp.sum(gates, axis=1)[:, None]


def shards(
    tokens, out_grad, expert_ids, route_gates, gate_weight, up_weight, down_weight, momentum
):
    token_count, model_width = tokens.shape
    topk_count = expert_ids.shape[1]
    peers, cores = lax.axis_size("ep"), lax.axis_size("opt")
    capacity = 2 * token_count * topk_count // peers
    slot_count = peers * capacity
    chosen, gates = placement(expert_ids, route_gates, slot_count, capacity)
    part = model_width // cores
    first = lax.axis_index("opt") * part
    part_tokens = lax.dynamic_slice_in_dim(tokens, first, part, 1)
    part_grads = lax.dynamic_slice_in_dim(out_grad, first, part, 1)
    send_inputs = jnp.dot(chosen, part_tokens, preferred_element_type=jnp.float32).astype(
        jnp.bfloat16
    )
    send_scaled = (
        gates * jnp.dot(chosen, part_grads, preferred_element_type=jnp.float32)
    ).astype(jnp.bfloat16)
    shape = (peers, capacity, part)
    recv_inputs, recv_scaled = dispatch(
        send_inputs.reshape(shape), send_scaled.reshape(shape), peers, cores
    )
    recv_inputs = recv_inputs.reshape(slot_count, model_width)
    recv_scaled = recv_scaled.reshape(slot_count, model_width)
    weight_gate = gate_weight[0]
    weight_up = up_weight[0]
    weight_down = down_weight[0]
    pre_gate = jnp.dot(recv_inputs, weight_gate, preferred_element_type=jnp.float32)
    pre_up = jnp.dot(recv_inputs, weight_up, preferred_element_type=jnp.float32)
    sigmoid = jax.nn.sigmoid(pre_gate)
    activated = pre_gate * sigmoid
    hidden = (activated * pre_up).astype(jnp.bfloat16)
    hidden_grad = lax.dot_general(
        recv_scaled, weight_down, CONTRACT_LAST, preferred_element_type=jnp.float32
    )
    gate_grad = (hidden_grad * pre_up * sigmoid * (1.0 + pre_gate * (1.0 - sigmoid))).astype(
        jnp.bfloat16
    )
    up_grad = (hidden_grad * activated).astype(jnp.bfloat16)
    partial_grad = lax.dot_general(
        gate_grad, weight_gate, CONTRACT_LAST, preferred_element_type=jnp.float32
    ) + lax.dot_general(up_grad, weight_up, CONTRACT_LAST, preferred_element_type=jnp.float32)
    partial_grad = partial_grad.astype(jnp.bfloat16).reshape(peers, capacity, model_width)
    down_grad = lax.dot_general(
        hidden, recv_scaled, CONTRACT_FIRST, preferred_element_type=jnp.float32
    )
    new_moment = momentum_decay * momentum[0] + down_grad
    squares = jnp.broadcast_to(jnp.sum(new_moment * new_moment), (8, 128))
    returned, own_rows = return_and_orthogonalize(partial_grad, new_moment, squares, cores)
    token_grad = lax.dot_general(
        chosen, returned.reshape(slot_count, part), CONTRACT_FIRST,
        preferred_element_type=jnp.float32,
    ).astype(jnp.bfloat16)
    update = math.sqrt(model_width) * own_rows.astype(jnp.float32)
    return (token_grad, new_moment[None], update[None])


def solution(mesh):
    in_specs = (
        P("ep", None),
        P("ep", None),
        P("ep", None),
        P("ep", None),
        P("ep", None, "opt"),
        P("ep", None, "opt"),
        P("ep", "opt", None),
        P("ep", "opt", None),
    )
    out_specs = (P("ep", "opt"), P("ep", "opt", None), P("ep", "opt", None))
    return jax.shard_map(shards, mesh=mesh, in_specs=in_specs, out_specs=out_specs, check_vma=False)
```

time: 197 us -> 118 us (0.60)
  Pallas kernels: 0 us -> 91.4 us
  blocking collectives: 63.8 us -> 0 us
  waiting for transfers between devices: 44.2 us -> 0 us
  matrix products: 38.9 us -> 16.6 us
  between operations: 14.7 us -> 0.73 us
  local copies, waits for them, and re-layouts: 14.8 us -> 4.81 us
  other arithmetic: 12.4 us -> 3.82 us
  starting transfers between devices: 7.29 us -> 0 us
    pallas_call x0 -> x2, Pallas kernels: none -> 91.4 us  [the longest x1 57 us: dispatch(): pl.pallas_call(functools.partial(dispatch_kernel, peers), out_shape=(out,...]
    all_to_all x2 -> x0, blocking collectives: 60.7 us -> none  [the longest x1 31.3 us: shards(): lax.all_to_all(send_inputs, 'ep', split_axis=0, concat_axis=0, tiled=True)]
    all_to_all x1 -> x0, waiting for transfers between devices: 36.4 us -> none  [shards(): lax.all_to_all(partial_grad.astype(jnp.bfloat16), 'ep', split_axis=0, con...]
    dot_general x10 -> x7, matrix products: 35.7 us -> 13.4 us  [the longest x1 2.76 us: shards(): lax.dot_general(hidden, recv_scaled, CONTRACT_FIRST, preferred_element_ty...]
    all_gather x3 -> x0, waiting for transfers between devices: 7.74 us -> none  [the longest x1 7.7 us: shards(): lax.all_gather(half_scaled, 'opt', axis=1, tiled=True)]
    all_to_all x1 -> x0, starting transfers between devices: 6.95 us -> none  [shards(): lax.all_to_all(partial_grad.astype(jnp.bfloat16), 'ep', split_axis=0, con...]
    gather x2 -> x0, local copies, waits for them, and re-layouts: 3.11 us -> none  [combine_rows(): returned[slots].astype(jnp.float32)]
    psum x1 -> x0, blocking collectives: 3.08 us -> none  [shards(): squares = lax.psum(jnp.sum(new_moment * new_moment), 'opt')]
  transfers between devices with their start and end apart: 5 -> 0, of which waited for: 2 -> 0; matrix products, arithmetic and copies ran while one was open for 24% -> 0% of each run, Pallas kernels for 0% -> 0%
where the time goes in v1:
time: 118 us; the launch traced here: 117 us
  Pallas kernels  91.4 us (77%)
  matrix products  16.6 us (14%)
  local copies, waits for them, and re-layouts  4.81 us (4%)
  other arithmetic  3.82 us (3%)
    pallas_call x1, Pallas kernels, dispatch(): pl.pallas_call(functools.partial(dispatch_kernel, peers), out_shape=(out,...  57 us
    pallas_call x1, Pallas kernels, return_and_orthogonalize(): pl.pallas_call(functools.partial(return_kernel, peers, groups), out_shape...  34.4 us
    broadcast_in_dim x1, other arithmetic, shards(): return (token_grad, new_moment[None], update[None])  2.8 us
    dot_general x1, matrix products, shards(): lax.dot_general(hidden, recv_scaled, CONTRACT_FIRST, preferred_element_ty...  2.76 us
    dot_general x1, matrix products, shards(): jnp.dot(recv_inputs, weight_gate, preferred_element_type=jnp.float32)  2.45 us
    dot_general x1, matrix products, shards(): jnp.dot(chosen, part_grads, preferred_element_type=jnp.float32)  2.36 us

profile of v1, /device:TPU:14, one launch (start us, length us, event | category | flops | bytes accessed | tf_op | source)
XLA Modules:
  0.0 117.4 jit_solution(3579605747095496121)
XLA Ops:
  0.6 0.0 copy-start
  0.6 0.8 slice_bitcast_fusion.1
  1.4 0.8 slice_bitcast_fusion.2
  2.2 0.1 convert_reduce_fusion.1
  2.3 0.8 multiply_add_fusion.1
  3.1 0.1 add_reduce_fusion
  3.2 2.4 %multiply_convert_fusion = bf16[512,1024]{1,0:T(8,128)(2,1)} fusion(f32[512]{0:T(512)S(1)} %add_reduce_fusion, bf16[128,2048]{1,0:T(8,128)(2,1)} %param.9, s32[]{:T(128)S(6)} %select_n.11, s32[128]{0:T(128)S(1)} %get-tuple-element.16, s32[128]{0:T(128)S(1)} %get-tuple-element.15), kind=kOutput, calls=%fused_computation.4 | convolution fusion | flops 135462912 | bytes 1313796 | tf_op jit(solution)/shard_map/dot_general | solution.py:359
  5.6 2.3 %convolution_convert_fusion = bf16[512,1024]{1,0:T(8,128)(2,1)} fusion(bf16[128,2048]{1,0:T(8,128)(2,1)} %param.8, s32[]{:T(128)S(6)} %select_n.11, s32[128]{0:T(128)S(1)} %get-tuple-element.16, s32[128]{0:T(128)S(1)} %get-tuple-element.15), kind=kOutput, calls=%fused_computation.5 | convolution fusion | flops 134938624 | bytes 1311748 | tf_op jit(solution)/shard_map/dot_general | solution.py:355
  7.9 57.0 %dispatch.1 = (bf16[16,32,2048]{2,1,0:T(8,128)(2,1)}, bf16[16,32,2048]{2,1,0:T(8,128)(2,1)}) custom-call(bf16[16,32,1024]{2,1,0:T(8,128)(2,1)} %bitcast.44, bf16[16,32,1024]{2,1,0:T(8,128)(2,1)} %bitcast.43), custom_call_target="tpu_custom_call" | custom-call | tf_op jit(solution)/shard_map/dispatch/pallas_call | solution.py:126
  65.0 0.0 copy-start.3
  65.0 0.0 copy-start.4
  65.0 0.0 copy-done
  65.0 2.5 %fusion.2 = f32[512,256]{1,0:T(8,128)S(1)} fusion(bf16[512,2048]{1,0:T(8,128)(2,1)} %bitcast.48, bf16[1,2048,256]{2,1,0:T(8,128)(2,1)S(1)} %copy-done), kind=kOutput, calls=%fused_computation.9 | convolution fusion | flops 536870912 | bytes 3670016 | tf_op jit(solution)/shard_map/dot_general | solution.py:370
  67.5 0.0 copy-done.3
  67.5 0.1 copy-done.4
  67.5 0.0 copy-start.2
  67.5 0.0 copy-start.5
  67.5 0.7 fusion.5
  68.3 0.8 copy-done.2
  69.1 0.3 copy-done.5
  69.4 0.0 copy-start.1
  69.4 0.7 fusion.7
  70.1 0.8 copy-done.1
  71.0 2.8 %multiply_reduce_fusion = (f32[]{:T(128)}, f32[256,2048]{1,0:T(8,128)}) fusion(bf16[512,2048]{1,0:T(8,128)(2,1)S(1)} %bitcast.46, f32[512,256]{1,0:T(8,128)S(1)} %fusion.5, f32[512,256]{1,0:T(8,128)S(1)} %fusion.2, f32[1,256,2048]{2,1,0:T(8,128)S(1)} %copy-done.1), kind=kOutput, calls=%fused_computation.3 | convolution fusion | flops 539754496 | bytes 7340036 | tf_op jit(solution)/shard_map/dot_general | solution.py:386
  73.7 1.2 %broadcast_in_dim.39.squares = f32[8,128]{1,0:T(8,128)} broadcast(f32[]{:T(128)} %get-tuple-element.19), dimensions={} | broadcast | bytes 4100 | tf_op jit(solution)/shard_map/broadcast_in_dim | solution.py:390
  75.0 0.8 fusion
  75.8 2.1 %add_convert_fusion = bf16[512,2048]{1,0:T(8,128)(2,1)} fusion(f32[512,2048]{1,0:T(8,128)S(1)} %fusion, bf16[1,2048,256]{2,1,0:T(8,128)(2,1)S(1)} %copy-done.3, f32[512,256]{1,0:T(8,128)S(1)} %fusion.7, f32[512,256]{1,0:T(8,128)S(1)} %fusion.2), kind=kOutput, calls=%fused_computation | convolution fusion | flops 539754496 | bytes 8388608 | tf_op jit(solution)/shard_map/dot_general | solution.py:384
  77.9 34.4 %return_ortho.1 = (bf16[16,32,1024]{2,1,0:T(8,128)(2,1)}, bf16[256,2048]{1,0:T(8,128)(2,1)}) custom-call(bf16[16,32,2048]{2,1,0:T(8,128)(2,1)} %bitcast.42, f32[256,2048]{1,0:T(8,128)} %get-tuple-element.20.moment, f32[8,128]{1,0:T(8,128)} %broadcast_in_dim.39.squares), custom_call_target="tpu_custom_call" | custom-call | tf_op jit(solution)/shard_map/return_ortho/pallas_call | solution.py:294
  112.3 2.3 %convolution_convert_fusion.1 = bf16[128,1024]{1,0:T(8,128)(2,1)} fusion(bf16[512,1024]{1,0:T(8,128)(2,1)} %bitcast.47, s32[128]{0:T(128)S(1)} %get-tuple-element.16, s32[128]{0:T(128)S(1)} %get-tuple-element.15), kind=kOutput, calls=%fused_computation.6 | convolution fusion | flops 134545408 | bytes 1311744 | tf_op jit(solution)/shard_map/dot_general | solution.py:392
  114.6 2.8 %multiply_bitcast_fusion = f32[1,256,2048]{2,1,0:T(8,128)} fusion(bf16[256,2048]{1,0:T(8,128)(2,1)} %get-tuple-element.10), kind=kLoop, calls=%fused_computation.2 | loop fusion | flops 1048576 | bytes 3145728 | tf_op jit(solution)/shard_map/broadcast_in_dim | solution.py:397
Async XLA Ops:
  0.6 64.4 %copy-start = (bf16[1,2048,256]{2,1,0:T(8,128)(2,1)S(1)}, bf16[1,2048,256]{2,1,0:T(8,128)(2,1)}, u32[]{:S(2)}) copy-start(bf16[1,2048,256]{2,1,0:T(8,128)(2,1)} %param.12) | copy-start | bytes 3145732
  65.0 2.5 %copy-start.3 = (bf16[1,2048,256]{2,1,0:T(8,128)(2,1)S(1)}, bf16[1,2048,256]{2,1,0:T(8,128)(2,1)}, u32[]{:S(2)}) copy-start(bf16[1,2048,256]{2,1,0:T(8,128)(2,1)} %param.13) | copy-start | bytes 3145732
  65.0 2.5 %copy-start.4 = (bf16[16,32,2048]{2,1,0:T(8,128)(2,1)S(1)}, bf16[16,32,2048]{2,1,0:T(8,128)(2,1)}, u32[]{:S(2)}) copy-start(bf16[16,32,2048]{2,1,0:T(8,128)(2,1)} %get-tuple-element.8) | copy-start | bytes 6291460
  67.5 1.6 %copy-start.2 = (bf16[16,32,2048]{2,1,0:T(8,128)(2,1)S(1)}, bf16[16,32,2048]{2,1,0:T(8,128)(2,1)}, u32[]{:S(2)}) copy-start(bf16[16,32,2048]{2,1,0:T(8,128)(2,1)} %get-tuple-element.7) | copy-start | bytes 6291460
  67.5 1.9 %copy-start.5 = (bf16[1,256,2048]{2,1,0:T(8,128)(2,1)S(1)}, bf16[1,256,2048]{2,1,0:T(8,128)(2,1)}, u32[]{:S(2)}) copy-start(bf16[1,256,2048]{2,1,0:T(8,128)(2,1)} %param.14) | copy-start | bytes 3145732
  69.4 1.6 %copy-start.1 = (f32[1,256,2048]{2,1,0:T(8,128)S(1)}, f32[1,256,2048]{2,1,0:T(8,128)}, u32[]{:S(2)}) copy-start(f32[1,256,2048]{2,1,0:T(8,128)} %param.15) | copy-start | bytes 6291460
